TPU v7x, 32 devices: a whole 2x2x4 slice. The times are simulated.
32 devices in a mesh: rows: 8 (over z, y), grp: 4 (over x, core).
Axes of the slice: x: 2, y: 2, z: 4, core: 2. Of those that a mesh axis runs over, the one named last changes fastest.
Arguments:
- hamiltonian: float32 [13824, 13824], P(('rows', 'grp')), as said below
- current: float32 [13824, 16], P(('rows', 'grp')), may hold values from -6 to 6
- previous: float32 [13824, 16], P(('rows', 'grp')), may hold values from -6 to 6
Outputs:
- new_current: float32 [13824, 16], P(('rows', 'grp'))
- new_previous: float32 [13824, 16], P(('rows', 'grp'))
- residual_rms: float32 [16], replicated
Inputs may be any that keep to these rules, and one draw needn't show every extreme that they name: hamiltonian is symmetric: hamiltonian[i, j] equals hamiltonian[j, i].
All inputs are finite; a program needn't handle non-finite values.
Results may differ from a plain program's by a relative error of at most 0.0003.
Values sent between devices are 32-bit elements; how exact they have to be, the bound alone decides.
A program may use at most 64 MiB of HBM per device.

v0:
```python
import math

import jax
import jax.numpy as jnp
from jax import lax
from jax.sharding import PartitionSpec as P

NEIG = 16
SIGN_STEPS = 6
ORDER = 13824


highest = lax.Precision.HIGHEST
eps_value = 1e-06


def mat_mul(left, right):
    return jnp.dot(left, right, precision=highest, preferred_element_type=jnp.float32)


def diag_of(matrix):
    mask = jnp.eye(matrix.shape[0], dtype=matrix.dtype)
    return jnp.sum(matrix * mask, axis=1)


def ritz_update(stiff, mass):
    stiff_sym = 0.5 * (stiff + stiff.T)
    lower = jnp.linalg.cholesky(mass)
    half_way = jax.scipy.linalg.solve_triangular(lower, stiff_sym, lower=True)
    reduced = jax.scipy.linalg.solve_triangular(lower, half_way.T, lower=True)
    identity = jnp.eye(reduced.shape[0], dtype=reduced.dtype)
    level = jnp.max(diag_of(reduced)[:NEIG])
    signed = level * identity - reduced
    signed = signed / jnp.sqrt(jnp.sum(signed * signed))
    for sweep_index in range(SIGN_STEPS):
        signed = 1.5 * signed - 0.5 * mat_mul(signed, mat_mul(signed, signed))
    projector = 0.5 * (identity + signed)
    coeffs = jax.scipy.linalg.solve_triangular(lower, projector[:, :NEIG], trans=1, lower=True)
    return coeffs * math.sqrt(ORDER)


def body(hamiltonian, current, previous):
    row_count = current.shape[0]
    offset = lax.axis_index(("rows", "grp")) * row_count
    own_block = lax.dynamic_slice_in_dim(hamiltonian, offset, row_count, 1)
    diag_vals = diag_of(own_block)

    def apply_ham(block):
        return mat_mul(hamiltonian, lax.all_gather(block, ("rows", "grp"), axis=0, tiled=True))

    paired = jnp.concatenate([current, previous], axis=1)
    hpaired = apply_ham(paired)
    image = hpaired[:, :NEIG]
    hprev = hpaired[:, NEIG:]
    cross_sum, gram_sum, image_sq = lax.psum(
        (mat_mul(current.T, image), mat_mul(current.T, current), jnp.sum(image * image, axis=0)),
        ("rows", "grp"),
    )
    ritz = cross_sum / ORDER
    resid = image - mat_mul(current, ritz)
    squares = (
        image_sq
        - 2.0 * jnp.sum(cross_sum * ritz, axis=0)
        + jnp.sum(ritz * mat_mul(gram_sum, ritz), axis=0)
    )
    residual_rms = jnp.sqrt(squares / ORDER + eps_value)
    shift = jnp.maximum(jnp.abs(diag_vals[:, None] - diag_of(ritz)[None, :]), 1.0)
    search = resid / (shift * residual_rms[None, :])
    hsearch = apply_ham(search)
    basis = jnp.concatenate([current, search, previous], axis=1)
    himage = jnp.concatenate([image, hsearch, hprev], axis=1)
    stiff, mass = lax.psum((mat_mul(basis.T, himage), mat_mul(basis.T, basis)), ("rows", "grp"))
    coeffs = ritz_update(stiff, mass)
    new_current = mat_mul(basis, coeffs)
    new_previous = mat_mul(basis[:, NEIG:], coeffs[NEIG:])
    return (new_current, new_previous, residual_rms)


def solution(mesh):
    return jax.shard_map(
        body,
        mesh=mesh,
        in_specs=(P(("rows", "grp"), None), P(("rows", "grp"), None), P(("rows", "grp"), None)),
        out_specs=(P(("rows", "grp"), None), P(("rows", "grp"), None), P()),
        check_vma=False,
    )
```

profile of v0, /device:TPU:1, one launch (start us, length us, event | category | flops | bytes accessed | tf_op | source)
XLA Modules:
  0.0 268.1 jit_solution(4251686484043219794)
XLA Ops:
  7.2 0.0 copy-start
  7.2 0.0 copy-start.1
  7.2 0.0 all-gather.4.cloned.1.call-start
  7.2 1.4 fusion.14
  8.6 0.0 all-gather.4.cloned.1.call-update
  8.7 1.5 select_reduce_fusion
  10.2 1.0 fusion.60
  11.1 58.4 %all-gather.4.cloned.1.call-done = f32[32,432,32]{1,2,0:T(8,128)} async-done(((f32[1,432,32]{1,2,0:T(8,128)}), f32[32,432,32]{1,2,0:T(8,128)}) %all-gather.4.cloned.1.call-update) | async-done | bytes 1769488 | tf_op jit(solution)/shard_map/all_gather | solution.py:49
  69.5 2.8 %copy.32 = f32[32,432,32]{1,0,2:T(8,128)S(1)} copy(f32[32,432,32]{1,2,0:T(8,128)} %all-gather.4.cloned.1.call-done) | data formatting | bytes 3538944 | tf_op jit(solution)/shard_map/all_gather | solution.py:49
  72.3 2.4 reshape.23
  74.8 24.7 %convolution_bitcast_fusion = f32[432,32]{0,1:T(8,128)S(1)} fusion(f32[13824,32]{0,1:T(8,128)} %reshape.23, f32[432,13824]{1,0:T(8,128)} %param.5), kind=kOutput, calls=%fused_computation | convolution fusion | flops 2293235712 | bytes 25712640 | tf_op jit(solution)/shard_map/dot_general | solution.py:18
  99.5 0.1 fusion.59
  99.6 0.0 copy-done
  99.6 0.1 convolution_bitcast_fusion.4
  99.7 37.7 %all-reduce.1 = (f32[16,16]{1,0:T(8,128)S(1)}, f32[16,16]{0,1:T(8,128)S(1)}, f32[16]{0:T(128)S(1)}) all-reduce(f32[16,16]{1,0:T(8,128)S(1)} %fusion.60, f32[16,16]{0,1:T(8,128)S(1)} %convolution_bitcast_fusion.4, f32[16]{0:T(128)S(1)} %get-tuple-element.12), channel_id=1, replica_groups=mesh['rows'=8,'grp'=4] {'rows','grp'}, use_global_device_ids=true, to_apply=%region_6.0 | all-reduce | flops 528 | bytes 4224 | tf_op jit(solution)/shard_map/psum | solution.py:55
  137.4 0.1 fusion.39
  137.5 0.2 fusion.7
  137.8 0.0 copy-start.2
  137.8 0.2 fusion.1
  138.0 0.0 copy-done.1
  138.0 0.2 fusion.18
  138.2 44.8 %all-gather.1 = f32[32,432,16]{1,2,0:T(8,128)S(1)} all-gather(f32[1,432,16]{1,2,0:T(8,128)S(1)} %bitcast.77), channel_id=1, replica_groups=mesh['rows'=8,'grp'=4] {'rows','grp'}, dimensions={0}, use_global_device_ids=true | all-gather | bytes 912384 | tf_op jit(solution)/shard_map/all_gather | solution.py:49
  183.0 0.6 copy.36
  183.6 0.6 reshape.25
  184.1 22.9 %convolution_bitcast_fusion.1 = f32[432,16]{0,1:T(8,128)S(1)} fusion(f32[13824,16]{0,1:T(8,128)S(1)} %reshape.25, f32[432,13824]{1,0:T(8,128)} %param.5), kind=kOutput, calls=%fused_computation.1 | convolution fusion | flops 1146617856 | bytes 24800256 | tf_op jit(solution)/shard_map/dot_general | solution.py:18
  207.1 0.2 fusion.8
  207.3 36.2 %all-reduce = (f32[48,48]{0,1:T(8,128)S(1)}, f32[48,48]{0,1:T(8,128)S(1)}) all-reduce(f32[48,48]{0,1:T(8,128)S(1)} %fusion.8, f32[48,48]{0,1:T(8,128)S(1)} %fusion.18), channel_id=1, replica_groups=mesh['rows'=8,'grp'=4] {'rows','grp'}, use_global_device_ids=true, to_apply=%region_11.12 | all-reduce | flops 4608 | bytes 36864 | tf_op jit(solution)/shard_map/psum | solution.py:72
  243.5 0.1 copy.35
  243.6 4.4 %cholesky.19 = f32[48,48]{1,0:T(8,128)S(1)} custom-call(f32[48,48]{1,0:T(8,128)S(1)} %fusion.30), custom_call_target="Cholesky" | custom-call | tf_op jit(solution)/shard_map/jit(cholesky)/cholesky | solution.py:28
  248.0 0.6 compare_reduce_fusion
  248.6 0.7 fusion.19
  249.3 3.7 %custom-call.10 = f32[1,48,48]{1,2,0:T(8,128)S(1)} custom-call(f32[1,48,48]{2,1,0:T(8,128)S(1)} %fusion.19), custom_call_target="InvertDiagBlocksLowerTriangular" | custom-call | tf_op jit(solution)/shard_map/jit(_solve_triangular)/triangular_solve | solution.py:38
  252.9 0.1 copy.38
  253.0 0.2 convolution_bitcast_fusion.3
  253.3 0.3 select_reduce_fusion.1
  253.6 0.6 slice_reduce_fusion
  254.2 1.3 multiply_reduce_fusion.1
  256.2 0.8 fusion.42
  257.0 0.8 fusion.6
  257.8 0.1 fusion.61
  257.9 0.2 fusion.5
  258.1 0.1 fusion.62
  258.3 0.2 fusion.4
  258.4 0.1 fusion.63
  258.6 0.2 fusion.3
  258.7 0.1 fusion.64
  258.9 0.2 fusion.2
  259.1 0.1 fusion.65
  259.2 0.2 fusion.66
  259.4 0.2 convolution_multiply_fusion.6
  259.6 0.9 fusion.15
  260.5 0.8 fusion.17
  261.3 0.0 copy-done.2
  (4 shorter events, 0.1 us)
Async XLA Ops:
  7.2 92.4 %copy-start = (f32[432,16]{0,1:T(8,128)S(1)}, f32[432,16]{0,1:T(8,128)}, u32[]{:S(2)}) copy-start(f32[432,16]{0,1:T(8,128)} %param.6) | copy-start | bytes 82948
  7.2 130.8 %copy-start.1 = (f32[432,16]{0,1:T(8,128)S(1)}, f32[432,16]{0,1:T(8,128)}, u32[]{:S(2)}) copy-start(f32[432,16]{0,1:T(8,128)} %param.7) | copy-start | bytes 82948
  7.2 62.3 %all-gather.4.cloned.1.call-start = ((), (), s32[]{:S(2)}) async-start(), calls=%async_computation | async-start | bytes 2162688 | tf_op jit(solution)/shard_map/all_gather | solution.py:49
  137.8 123.5 %copy-start.2 = (f32[16]{0:T(128)}, f32[16]{0:T(128)S(1)}, u32[]{:S(2)}) copy-start(f32[16]{0:T(128)S(1)} %add_sqrt_fusion) | copy-start | bytes 196
Sparse Core Ops, SparseCore 0:
  10.9 58.6 all-gather.3
where the time goes:
time: 271 us; the launch traced here: 268 us
  blocking collectives  119 us (44%)
  waiting for transfers between devices  58.4 us (22%)
  matrix products  55.1 us (20%)
  between operations  15 us (6%)
  other arithmetic  14.4 us (5%)
  local copies, waits for them, and re-layouts  6.56 us (2%)
    all_gather x1, waiting for transfers between devices, apply_ham(): lax.all_gather(block, ('rows', 'grp'), axis=0, tiled=True)  58.4 us
    dot_general x22, matrix products, mat_mul(): jnp.dot(left, right, precision=highest, preferred_element_type=jnp.float32)  54.4 us
    all_gather x1, blocking collectives, apply_ham(): lax.all_gather(block, ('rows', 'grp'), axis=0, tiled=True)  44.8 us
    psum x1, blocking collectives, body(): lax.psum((mat_mul(current.T, image), mat_mul(current.T, current), jnp.sum...  37.7 us
    psum x1, blocking collectives, body(): lax.psum((mat_mul(basis.T, himage), mat_mul(basis.T, basis)), ('rows', 'g...  36.2 us
  transfers between devices with their start and end apart: 1, of which 1 were waited for; matrix products, arithmetic and copies ran while one was open for 1% of the time, Pallas kernels for 0%

commit v1 on v0

v1 whole, which is shorter than its diff:
```python
import functools
import math

import jax
import jax.numpy as jnp
from jax import lax
from jax.experimental import pallas as pl
from jax.experimental.pallas import tpu as pltpu
from jax.sharding import PartitionSpec as P

SIGN_STEPS = 6
EPS = 1e-06
MESH = pl.DeviceIdType.MESH
F32 = jnp.float32
BF16 = jnp.bfloat16
NT = (((1,), (1,)), ((), ()))
NN = (((1,), (0,)), ((), ()))


def dot_hi(a, b, dims=NN):
    return lax.dot_general(a, b, dims, precision=lax.Precision.HIGHEST, preferred_element_type=F32)


def dot_bf(a, b, dims=NN):
    return lax.dot_general(a, b, dims, preferred_element_type=F32)


def split(x):
    hi = x.astype(BF16)
    return hi, (x - hi.astype(F32)).astype(BF16)


def iota(shape, axis):
    return lax.broadcasted_iota(jnp.int32, shape, axis)


def kernel(R, G, rows, K, n, T, MW,
           h_ref, cur_ref, prev_ref, nc_ref, np_ref, rms_ref,
           hf, hhi, hlo, b1, b2, b3, b4, b5, vc, vp, vi, vbc, vbp, vbs, acc, basis, rhs, tr,
           hsem, ss, rs, fs, fr):
    half = G // 2
    C = R * half
    D = 2 * C
    W = MW + 128
    TK = K // T
    r = lax.axis_index("rows")
    g = lax.axis_index("grp")
    core = lax.rem(g, 2)
    chip = r * half + g // 2
    dev = 2 * chip + core

    def ident(q, k):
        return (q // half, lax.rem(q, half) * 2 + k)

    for t in range(T):
        cs = slice(t * TK, (t + 1) * TK)
        pltpu.make_async_copy(h_ref.at[:, cs], hf.at[:, cs], hsem.at[t]).start()

    barrier = pltpu.get_barrier_semaphore()

    def greet(p, _):
        pl.semaphore_signal(barrier, inc=1, device_id=ident(lax.rem(chip + p, C), core), device_id_type=MESH)
        return 0

    lax.fori_loop(1, C, greet, 0)
    pl.semaphore_signal(barrier, inc=1, device_id=ident(chip, 1 - core), device_id_type=MESH)
    pl.semaphore_wait(barrier, C)

    def direct(m, buf, src, p):
        return pltpu.make_async_remote_copy(
            src_ref=src, dst_ref=buf.at[dev], send_sem=ss.at[m, p], recv_sem=rs.at[m, chip],
            device_id=ident(lax.rem(chip + p, C), core), device_id_type=MESH)

    def arrive(m, buf, q):
        return pltpu.make_async_remote_copy(
            src_ref=buf.at[2 * q + core], dst_ref=buf.at[2 * q + core], send_sem=ss.at[m, 0],
            recv_sem=rs.at[m, q], device_id=ident(q, core), device_id_type=MESH)

    def forward(m, buf, q, src):
        return pltpu.make_async_remote_copy(
            src_ref=src, dst_ref=buf.at[2 * q + core], send_sem=fs.at[m, q], recv_sem=fr.at[m, q],
            device_id=ident(chip, 1 - core), device_id_type=MESH)

    def send(m, buf, src=None):
        src = buf.at[dev] if src is None else src

        def one(p, _):
            direct(m, buf, src, p).start()
            return 0

        lax.fori_loop(1, C, one, 0)
        forward(m, buf, chip, src).start()

    def relay(m, buf):
        def one(p, _):
            q = lax.rem(chip + C - p, C)
            arrive(m, buf, q).wait_recv()
            forward(m, buf, q, buf.at[2 * q + core]).start()
            return 0

        lax.fori_loop(1, C, one, 0)

    def collect(m, buf):
        def one(q, _):
            pltpu.make_async_remote_copy(
                src_ref=buf.at[2 * q + 1 - core], dst_ref=buf.at[2 * q + 1 - core], send_sem=fs.at[m, q],
                recv_sem=fr.at[m, q], device_id=ident(chip, 1 - core), device_id_type=MESH).wait_recv()
            return 0

        lax.fori_loop(0, C, one, 0)

    def drain(m, buf):
        def one(p, _):
            direct(m, buf, buf.at[dev], p).wait_send()
            return 0

        lax.fori_loop(1, C, one, 0)

        def two(q, _):
            forward(m, buf, q, buf.at[2 * q + core]).wait_send()
            return 0

        lax.fori_loop(0, C, two, 0)

    def assemble(buf, dst, masked):
        height = dst.shape[0]
        dst[...] = jnp.zeros_like(dst)
        keep = iota((height, MW), 1) < rows
        pad = jnp.zeros((height, 128), F32)
        for d in range(D):
            start = d * rows // 128 * 128
            x = buf[d]
            if masked:
                x = jnp.where(keep, x, 0.0)
            x = jnp.concatenate([x, pad], axis=1)
            shift = d * rows - start
            if shift:
                x = pltpu.roll(x, shift, 1)
            dst[:, start:start + W] += x

    def split_into(vb, v):
        hi, lo = split(v[0:n, 0:K])
        vb[0:n, :] = hi
        vb[n:2 * n, :] = lo

    def apply_ham(vb, first, last):
        def one(t, _):
            cols = pl.ds(pl.multiple_of(t * TK, 128), TK)
            v = vb[:, cols]
            acc[0:rows, 0:2 * n] += dot_bf(hhi[:, cols], v, NT) + dot_bf(hlo[:, cols], v, NT)
            return 0

        lax.fori_loop(first, last, one, 0)

    def clear():
        acc[...] = jnp.zeros_like(acc)

    def product():
        flat = acc[...].T
        return flat[0:n, :] + flat[n:2 * n, :]

    b1[dev] = cur_ref[...]
    send(0, b1, cur_ref)
    for t in range(T):
        cs = slice(t * TK, (t + 1) * TK)
        pltpu.make_async_copy(h_ref.at[:, cs], hf.at[:, cs], hsem.at[t]).wait()

        def part(s, _, t=t):
            cols = pl.ds(pl.multiple_of(t * TK + s * 128, 128), 128)
            hi, lo = split(hf[:, cols])
            hhi[:, cols] = hi
            hlo[:, cols] = lo
            return 0

        lax.fori_loop(0, TK // 128, part, 0)
    relay(0, b1)

    base = dev * rows // 128 * 128
    shift = dev * rows - base
    window = hf[:, pl.ds(pl.multiple_of(base, 128), W)]
    on_diag = iota((rows, W), 1) == iota((rows, W), 0) + shift
    own_diag = jnp.sum(jnp.where(on_diag, window, 0.0), axis=0, keepdims=True)
    own_diag = pltpu.roll(jnp.broadcast_to(own_diag, (8, W)), lax.rem(W - shift, W), 1)[:, 0:MW]
    b2[dev, 0:n, :] = prev_ref[...]
    b2[dev, n:n + 8, :] = own_diag
    send(1, b2)

    collect(0, b1)
    assemble(b1, vc, False)
    split_into(vbc, vc)
    clear()
    apply_ham(vbc, 0, T)
    image = product()
    cur = cur_ref[...]
    prev = prev_ref[...]
    cross = dot_hi(image, cur, NT)
    wide = jnp.concatenate([jnp.zeros((n, rows), F32), cross], axis=1)
    wide = jnp.concatenate([wide, jnp.zeros((n, MW - rows - n), F32)], axis=1)
    b3[dev] = image + wide
    send(2, b3)

    relay(1, b2)
    collect(1, b2)
    assemble(b2, vp, False)
    split_into(vbp, vp)
    clear()
    cut = (2 * T) // 3
    apply_ham(vbp, 0, cut)
    relay(2, b3)
    apply_ham(vbp, cut, T)
    hprev = product()
    collect(2, b3)

    tail = jnp.zeros((n, 128), F32)
    for d in range(D):
        tail = tail + b3[d, :, MW - 128:MW]
    tail = pltpu.roll(tail, (MW - rows) % 128, 1)
    tail = jnp.where(iota((n, 128), 1) < n, tail, 0.0)
    ritz = tail / K
    ritz_diag = jnp.sum(jnp.where(iota((n, 128), 0) == iota((n, 128), 1), ritz, 0.0), axis=1, keepdims=True)
    twice_hi, twice_lo = split(ritz + pltpu.roll(ritz, n, 1))
    twice_hi = twice_hi[:, 0:2 * n]
    twice_lo = twice_lo[:, 0:2 * n]
    assemble(b3, vi, True)

    def search_part(t, total):
        cols = pl.ds(pl.multiple_of(t * TK, 128), TK)
        v = vbc[:, cols]
        resid = vi[:, cols] - (dot_bf(twice_hi, v) + dot_bf(twice_lo, v))
        shifts = jnp.maximum(jnp.abs(vp[n:n + 1, cols] - ritz_diag), 1.0)
        hi, lo = split(resid / shifts)
        vbs[0:n, cols] = hi
        vbs[n:2 * n, cols] = lo
        return total + jnp.sum(resid * resid, axis=1, keepdims=True)

    total = lax.fori_loop(0, T, search_part, jnp.zeros((n, 1), F32))
    rms = jnp.sqrt(total / K + EPS)
    rms_ref[...] = jnp.broadcast_to(rms, (n, 128))

    resid = image - dot_hi(ritz[:, 0:n], cur)
    shifts = jnp.maximum(jnp.abs(own_diag[0:1, :] - ritz_diag), 1.0)
    basis[0:n, :] = cur
    basis[n:2 * n, :] = resid / (shifts * rms)
    basis[2 * n:3 * n, :] = prev
    rhs[...] = jnp.zeros_like(rhs)
    rhs[0:n, :] = image
    rhs[2 * n:3 * n, :] = hprev
    rhs[4 * n:7 * n, :] = basis[...]
    b4[dev] = dot_hi(basis[...], rhs[...], NT)
    send(3, b4)

    clear()
    apply_ham(vbs, 0, cut)
    relay(3, b4)
    apply_ham(vbs, cut, T)
    hsearch = product() / rms
    rhs[0:3 * n, :] = basis[...]
    b5[dev] = dot_hi(hsearch, rhs[...], NT)
    send(4, b5)

    collect(3, b4)
    sums = b4[0]
    for d in range(1, D):
        sums = sums + b4[d]
    N3 = 3 * n
    row_id = iota((N3, 128), 0)
    lane_id = iota((N3, 128), 1)
    work = jnp.where(lane_id < 4 * n, pltpu.roll(sums, 4 * n, 1), 0.0)
    work = jnp.where(lane_id == row_id + 4 * n, 1.0, work)
    for k in range(N3):
        pivot_row = work[k:k + 1, :] / work[k:k + 1, k:k + 1]
        factor = jnp.where(row_id > k, work[:, k:k + 1], 0.0)
        work = work - factor * pivot_row
    pivots = jnp.sum(jnp.where(row_id == lane_id, work, 0.0), axis=1, keepdims=True)
    work = work / jnp.sqrt(pivots)
    inverse = pltpu.roll(work, 4 * n, 1)[:, 0:N3]

    relay(4, b5)
    collect(4, b5)
    last = b5[0]
    for d in range(1, D):
        last = last + b5[d]
    tr[0:128, 0:128] = jnp.zeros((128, 128), F32)
    tr[n:2 * n, 0:128] = last
    stiff = jnp.where(lane_id < N3, sums, 0.0) + tr[0:128, 0:128].T[0:N3, :]
    tr[0:128, 0:128] = jnp.zeros((128, 128), F32)
    tr[0:N3, 0:128] = stiff
    stiff = (0.5 * (stiff + tr[0:128, 0:128].T[0:N3, :]))[:, 0:N3]
    reduced = dot_hi(dot_hi(inverse, stiff), inverse, NT)
    eye = jnp.where(iota((N3, N3), 0) == iota((N3, N3), 1), 1.0, 0.0).astype(F32)
    ours = (iota((N3, N3), 0) == iota((N3, N3), 1)) & (iota((N3, N3), 0) < n)
    level = jnp.max(jnp.where(ours, reduced, -jnp.inf), keepdims=True)
    signed = level * eye - reduced
    signed = signed / jnp.sqrt(jnp.sum(signed * signed, keepdims=True))
    for _ in range(SIGN_STEPS):
        signed = 1.5 * signed - 0.5 * dot_hi(signed, dot_hi(signed, signed))
    projector = 0.5 * (eye + signed)
    coeffs = dot_hi(projector[0:n, :], inverse) * math.sqrt(K)
    nc_ref[...] = dot_hi(coeffs, basis[...])
    np_ref[...] = dot_hi(jnp.where(iota((n, N3), 1) >= n, coeffs, 0.0), basis[...])

    for m, buf in enumerate((b1, b2, b3, b4, b5)):
        drain(m, buf)


def body(R, G, hamiltonian, current, previous):
    rows, n = current.shape
    K = hamiltonian.shape[1]
    C = R * G // 2
    D = 2 * C
    T = 9
    MW = -(-(rows + n) // 128) * 128
    W = MW + 128
    TW = max(MW, 128)
    pad = ((0, 0), (0, MW - rows))
    cur_t = jnp.pad(current.T, pad)
    prev_t = jnp.pad(previous.T, pad)
    vm = pl.BlockSpec(memory_space=pltpu.VMEM)
    nc, np_, rms = pl.pallas_call(
        functools.partial(kernel, R, G, rows, K, n, T, MW),
        out_shape=[jax.ShapeDtypeStruct((n, MW), F32), jax.ShapeDtypeStruct((n, MW), F32),
                   jax.ShapeDtypeStruct((n, 128), F32)],
        in_specs=[pl.BlockSpec(memory_space=pl.ANY), vm, vm],
        out_specs=[vm, vm, vm],
        scratch_shapes=[
            pltpu.VMEM((rows, K + 128), F32),
            pltpu.VMEM((rows, K), BF16),
            pltpu.VMEM((rows, K), BF16),
            pltpu.VMEM((D, n, MW), F32),
            pltpu.VMEM((D, n + 8, MW), F32),
            pltpu.VMEM((D, n, MW), F32),
            pltpu.VMEM((D, 3 * n, 128), F32),
            pltpu.VMEM((D, n, 128), F32),
            pltpu.VMEM((n, K + 128), F32),
            pltpu.VMEM((n + 8, K + 128), F32),
            pltpu.VMEM((n, K + 128), F32),
            pltpu.VMEM((2 * n, K), BF16),
            pltpu.VMEM((2 * n, K), BF16),
            pltpu.VMEM((2 * n, K), BF16),
            pltpu.VMEM((MW, 128), F32),
            pltpu.VMEM((3 * n, MW), F32),
            pltpu.VMEM((128, MW), F32),
            pltpu.VMEM((128, TW), F32),
            pltpu.SemaphoreType.DMA((T,)),
            pltpu.SemaphoreType.DMA((5, C)),
            pltpu.SemaphoreType.DMA((5, C)),
            pltpu.SemaphoreType.DMA((5, C)),
            pltpu.SemaphoreType.DMA((5, C)),
        ],
        compiler_params=pltpu.CompilerParams(
            collective_id=0, has_side_effects=True, vmem_limit_bytes=64000000),
    )(hamiltonian, cur_t, prev_t)
    return nc[:, :rows].T, np_[:, :rows].T, rms[:, 0]


def solution(mesh):
    R, G = mesh.shape["rows"], mesh.shape["grp"]
    spec = P(("rows", "grp"), None)
    return jax.shard_map(
        functools.partial(body, R, G),
        mesh=mesh,
        in_specs=(spec, spec, spec),
        out_specs=(spec, spec, P()),
        check_vma=False,
    )
```

time: 271 us -> 91.4 us (0.34)
  blocking collectives: 119 us -> 0 us
  Pallas kernels: 0 us -> 84.8 us
  waiting for transfers between devices: 58.4 us -> 0 us
  matrix products: 55.1 us -> 0 us
  other arithmetic: 14.4 us -> 0 us
  between operations: 15 us -> 0.64 us
    pallas_call x0 -> x1, Pallas kernels: none -> 84.8 us  [body(): pl.pallas_call(functools.partial(kernel, R, G, rows, K, n, T, MW), out_sh...]
    psum x2 -> x0, blocking collectives: 73.8 us -> none  [the longest x1 37.7 us: body(): lax.psum((mat_mul(current.T, image), mat_mul(current.T, current), jnp.sum...]
    all_gather x1 -> x0, waiting for transfers between devices: 58.4 us -> none  [apply_ham(): lax.all_gather(block, ('rows', 'grp'), axis=0, tiled=True)]
    dot_general x22 -> x0, matrix products: 54.4 us -> none  [mat_mul(): jnp.dot(left, right, precision=highest, preferred_element_type=jnp.float32)]
    all_gather x1 -> x0, blocking collectives: 44.8 us -> none  [apply_ham(): lax.all_gather(block, ('rows', 'grp'), axis=0, tiled=True)]
    another operation x6 -> x0, other arithmetic: 9.39 us -> none  [the longest x4 5.06 us: ritz_update(): lower = jnp.linalg.cholesky(mass)]
    all_gather x2 -> x0, local copies, waits for them, and re-layouts: 3.42 us -> none  [apply_ham(): lax.all_gather(block, ('rows', 'grp'), axis=0, tiled=True)]
    unnamed x8 -> x0, local copies, waits for them, and re-layouts: 2.98 us -> none
  transfers between devices with their start and end apart: 1 -> 0, of which waited for: 1 -> 0; matrix products, arithmetic and copies ran while one was open for 1% -> 0% of each run, Pallas kernels for 0% -> 0%
where the time goes in v1:
time: 91.4 us; the launch traced here: 91 us
  Pallas kernels  84.8 us (93%)
  local copies, waits for them, and re-layouts  5.48 us (6%)
    pallas_call x1, Pallas kernels, body(): pl.pallas_call(functools.partial(kernel, R, G, rows, K, n, T, MW), out_sh...  84.8 us

profile of v1, /device:TPU:1, one launch (start us, length us, event | category | flops | bytes accessed | tf_op | source)
XLA Modules:
  0.0 91.0 jit_solution(9406465606607142454)
XLA Ops:
  0.6 1.4 %pad.7.cur_ref = f32[16,512]{1,0:T(8,128)} pad(f32[16,432]{1,0:T(8,128)} %bitcast.6, f32[]{:T(128)} %constant.2.clone.1), padding=0_0x0_80 | pad | bytes 60420 | tf_op jit(solution)/shard_map/jit(_pad)/pad | solution.py:316
  2.0 1.4 %pad.8.prev_ref = f32[16,512]{1,0:T(8,128)} pad(f32[16,432]{1,0:T(8,128)} %bitcast.7, f32[]{:T(128)} %constant.2.clone.1), padding=0_0x0_80 | pad | bytes 60420 | tf_op jit(solution)/shard_map/jit(_pad)/pad | solution.py:317
  3.4 84.8 %shard_map.58 = (f32[16,512]{1,0:T(8,128)}, f32[16,512]{1,0:T(8,128)}, f32[16,128]{1,0:T(8,128)}) custom-call(f32[432,13824]{1,0:T(8,128)} %h_ref.1, f32[16,512]{1,0:T(8,128)} %pad.7.cur_ref, f32[16,512]{1,0:T(8,128)} %pad.8.prev_ref), custom_call_target="tpu_custom_call" | custom-call | tf_op jit(solution)/shard_map/pallas_call | solution.py:319
  88.2 1.4 %slice_bitcast_fusion = (f32[432,16]{0,1:T(8,128)}, f32[432,16]{0,1:T(8,128)}) fusion(f32[16,512]{1,0:T(8,128)} %get-tuple-element.7, f32[16,512]{1,0:T(8,128)} %get-tuple-element.6), kind=kLoop, calls=%fused_computation | loop fusion | bytes 110592 | tf_op jit(solution)/shard_map/transpose | solution.py:353
  89.6 1.3 %slice_reduce_fusion = f32[16]{0:T(128)} fusion(f32[16,128]{1,0:T(8,128)} %get-tuple-element.8), kind=kLoop, calls=%fused_computation.2 | loop fusion | bytes 128 | tf_op jit(solution)/shard_map/slice | solution.py:353

commit v2 on v1

--- a/solution.py
+++ b/solution.py
@@ -147,7 +147,7 @@
         def one(t, _):
             cols = pl.ds(pl.multiple_of(t * TK, 128), TK)
             v = vb[:, cols]
-            acc[0:rows, 0:2 * n] += dot_bf(hhi[:, cols], v, NT) + dot_bf(hlo[:, cols], v, NT)
+            acc[:, 0:rows] += dot_bf(v, hhi[:, cols], NT) + dot_bf(v, hlo[:, cols], NT)
             return 0
 
         lax.fori_loop(first, last, one, 0)
@@ -156,8 +156,7 @@
         acc[...] = jnp.zeros_like(acc)
 
     def product():
-        flat = acc[...].T
-        return flat[0:n, :] + flat[n:2 * n, :]
+        return acc[0:n, :] + acc[n:2 * n, :]
 
     b1[dev] = cur_ref[...]
     send(0, b1, cur_ref)
@@ -337,7 +336,7 @@
             pltpu.VMEM((2 * n, K), BF16),
             pltpu.VMEM((2 * n, K), BF16),
             pltpu.VMEM((2 * n, K), BF16),
-            pltpu.VMEM((MW, 128), F32),
+            pltpu.VMEM((2 * n, MW), F32),
             pltpu.VMEM((3 * n, MW), F32),
             pltpu.VMEM((128, MW), F32),
             pltpu.VMEM((128, TW), F32),

time: 91.4 us -> 91.4 us (level)
  no operation moved by 1% of the time
where the time goes in v2:
time: 91.4 us; the launch traced here: 90.9 us
  Pallas kernels  84.8 us (93%)
  local copies, waits for them, and re-layouts  5.48 us (6%)
    pallas_call x1, Pallas kernels, body(): pl.pallas_call(functools.partial(kernel, R, G, rows, K, n, T, MW), out_sh...  84.8 us

profile of v2, /device:TPU:1, one launch (start us, length us, event | category | flops | bytes accessed | tf_op | source)
XLA Modules:
  0.0 90.9 jit_solution(8924367496461809190)
XLA Ops:
  0.6 1.4 %pad.7.cur_ref = f32[16,512]{1,0:T(8,128)} pad(f32[16,432]{1,0:T(8,128)} %bitcast.6, f32[]{:T(128)} %constant.2.clone.1), padding=0_0x0_80 | pad | bytes 60420 | tf_op jit(solution)/shard_map/jit(_pad)/pad | solution.py:315
  2.0 1.4 %pad.8.prev_ref = f32[16,512]{1,0:T(8,128)} pad(f32[16,432]{1,0:T(8,128)} %bitcast.7, f32[]{:T(128)} %constant.2.clone.1), padding=0_0x0_80 | pad | bytes 60420 | tf_op jit(solution)/shard_map/jit(_pad)/pad | solution.py:316
  3.4 84.8 %shard_map.58 = (f32[16,512]{1,0:T(8,128)}, f32[16,512]{1,0:T(8,128)}, f32[16,128]{1,0:T(8,128)}) custom-call(f32[432,13824]{1,0:T(8,128)} %h_ref.1, f32[16,512]{1,0:T(8,128)} %pad.7.cur_ref, f32[16,512]{1,0:T(8,128)} %pad.8.prev_ref), custom_call_target="tpu_custom_call" | custom-call | tf_op jit(solution)/shard_map/pallas_call | solution.py:318
  88.2 1.4 %slice_bitcast_fusion = (f32[432,16]{0,1:T(8,128)}, f32[432,16]{0,1:T(8,128)}) fusion(f32[16,512]{1,0:T(8,128)} %get-tuple-element.7, f32[16,512]{1,0:T(8,128)} %get-tuple-element.6), kind=kLoop, calls=%fused_computation | loop fusion | bytes 110592 | tf_op jit(solution)/shard_map/transpose | solution.py:352
  89.6 1.3 %slice_reduce_fusion = f32[16]{0:T(128)} fusion(f32[16,128]{1,0:T(8,128)} %get-tuple-element.8), kind=kLoop, calls=%fused_computation.2 | loop fusion | bytes 128 | tf_op jit(solution)/shard_map/slice | solution.py:352
